TPU v7x, 512 devices: a whole 4x8x8 slice. The times are simulated.
512 devices in a mesh: tile: 32 (over z, y_hi), col: 16 (over x, y_lo, core).
Axes of the slice: x: 4, y: 8 (y_hi: 4, y_lo: 2; y = y_hi * 2 + y_lo), z: 8, core: 2. Of those that a mesh axis runs over, the one named last changes fastest.
Arguments:
- latent: bfloat16 [32, 17, 4, 64, 256], P('tile', None, None, 'col'), may hold values from -20 to 20
- intersections: int32 [32], P('tile'), may hold values from 0 to 4, as said below
- norm_gain_one: float32 [256], replicated, may hold values from 0.5 to 1.5
- norm_shift_one: float32 [256], replicated, may hold values from -3 to 3
- weight_one: bfloat16 [3, 3, 3, 256, 256], P(None, None, None, 'col'), may hold values from -0.078125 to 0.078125
- norm_gain_two: float32 [256], replicated, may hold values from 0.5 to 1.5
- norm_shift_two: float32 [256], replicated, may hold values from -3 to 3
- weight_two: bfloat16 [3, 3, 3, 256, 256], P(None, None, None, 'col'), may hold values from -0.078125 to 0.078125
- conv_bias: float32 [256], replicated, may hold values from -1.8 to 1.8
Outputs:
- blended: bfloat16 [32, 17, 4, 64, 256], P('tile', None, None, 'col')
Inputs may be any that keep to these rules, and one draw needn't show every extreme that they name: intersections[0] is 0 and every other entry is 1 to 4; some entry equals 4.
All inputs are finite; a program needn't handle non-finite values.
Results may differ from a plain program's by a relative error of at most 0.0055.
Values may be sent and summed in bfloat16 or wider, within the bound.
No kernel may reach another device: no remote copies, remote signals or barrier semaphores. Data moves between devices by JAX's collectives and lax.ppermute only.
A program may use at most 64 MiB of HBM per device.

v0:
```python
import jax
import jax.numpy as jnp
from jax import lax
from jax.sharding import PartitionSpec as P

GROUPS = 32
OVMAX = 4
epsilon = 1e-06


def copy_for_each(array, axis):
    copies = jnp.broadcast_to(array, (lax.axis_size(axis), *array.shape))
    return lax.all_to_all(copies, axis, split_axis=0, concat_axis=0, tiled=True)


def over_copies(array, axis):
    return copy_for_each(array, axis).sum(axis=0)


def together(arrays, axis):
    flat, at, gathered = (jnp.concatenate([a.reshape(-1) for a in arrays]), 0, [])
    so_far = over_copies(flat, axis)
    for a in arrays:
        gathered.append(so_far[at : at + a.size].reshape(a.shape))
        at += a.size
    return tuple(gathered)


def extended_2(array, sides, width):
    for axis, dim in sides:
        size, length = (lax.axis_size(axis), array.shape[dim])
        up = [(i, (i + 1) % size) for i in range(size - 1)]
        down = [(j, i) for i, j in up]
        last = lax.slice_in_dim(array, length - width, length, axis=dim)
        first = lax.slice_in_dim(array, 0, width, axis=dim)
        before = lax.ppermute(last, axis, up)
        after = lax.ppermute(first, axis, down)
        array = jnp.concatenate([before, array, after], axis=dim)
    return array


def shifted(block, axis, distance):
    devices = range(lax.axis_size(axis))
    route = [(i - distance, i) for i in devices if i - distance in devices]
    return lax.ppermute(block, axis, route)


def conv_taps(padded, kernel):
    frames = padded.shape[0]
    height = padded.shape[1]
    out_width = padded.shape[2] - 2
    channels = padded.shape[3]
    outputs = kernel.shape[4]
    padded = jnp.pad(padded, ((2, 0), (1, 1), (0, 0), (0, 0)))
    running = jnp.zeros((frames * height * out_width, outputs), jnp.float32)
    for tap_t in range(3):
        for tap_h in range(3):
            for tap_w in range(3):
                window = padded[
                    tap_t : tap_t + frames, tap_h : tap_h + height, tap_w : tap_w + out_width
                ]
                running = running + jnp.dot(
                    window.reshape(-1, channels),
                    kernel[tap_t, tap_h, tap_w],
                    preferred_element_type=jnp.float32,
                )
    return running.reshape(frames, height, out_width, outputs)


def group_total(values, per_group):
    return jnp.sum(values, axis=(0, 1, 2)).reshape(GROUPS, per_group).sum(axis=1)


def norm_silu(values, inner, gain, shift):
    channels = values.shape[3]
    per_group = channels // GROUPS
    members = inner.shape[0] * inner.shape[1] * inner.shape[2] * lax.axis_size("col") * per_group
    chan_sums = group_total(inner, per_group)
    chan_squares = group_total(inner * inner, per_group)
    totals, squares = together((chan_sums, chan_squares), "col")
    group_mean = totals / members
    spread = jnp.maximum(squares / members - group_mean * group_mean, 0.0)
    inv_std = lax.rsqrt(spread + epsilon)
    normed = (values - jnp.repeat(group_mean, per_group)) * jnp.repeat(
        inv_std, per_group
    ) * gain + shift
    return jax.nn.silu(normed).astype(jnp.bfloat16)


def shards(
    latent,
    intersections,
    norm_gain_one,
    norm_shift_one,
    weight_one,
    norm_gain_two,
    norm_shift_two,
    weight_two,
    conv_bias,
):
    source = latent[0]
    latent_full = source.astype(jnp.float32)
    act_one = norm_silu(latent_full, latent_full, norm_gain_one, norm_shift_one)
    kernel_one, kernel_two = (
        lax.all_gather(weight_one, "col", axis=3, tiled=True),
        lax.all_gather(weight_two, "col", axis=3, tiled=True),
    )
    margin = extended_2(act_one, (("col", 2),), 2)
    hidden = conv_taps(margin, kernel=kernel_one).astype(jnp.bfloat16)
    hidden_full = hidden.astype(jnp.float32)
    act_two = norm_silu(hidden_full, hidden_full[:, :, 1:-1], norm_gain_two, norm_shift_two)
    own_width = source.shape[2]
    position = lax.axis_index("col") * own_width - 1 + jnp.arange(own_width + 2, dtype=jnp.int32)
    inside = (position >= 0) & (position < own_width * lax.axis_size("col"))
    act_two = jnp.where(inside[None, None, :, None], act_two, jnp.zeros_like(act_two))
    branch = conv_taps(act_two, kernel=kernel_two)
    decoded = (latent_full + (branch + conv_bias)).astype(jnp.bfloat16)
    frames = decoded.shape[0]
    received = shifted(decoded[frames - OVMAX :], "tile", 1)
    shared = intersections[0]
    extended = jnp.concatenate([received, jnp.zeros_like(received)], axis=0)
    aligned = lax.dynamic_slice_in_dim(extended, OVMAX - shared, OVMAX, 0)
    position_t = jnp.arange(OVMAX, dtype=jnp.int32)
    own_share = ((position_t + 1).astype(jnp.float32) / (shared + 1).astype(jnp.float32))[
        :, None, None, None
    ]
    head = decoded[:OVMAX].astype(jnp.float32)
    active = (position_t < shared)[:, None, None, None]
    mixed = jnp.where(
        active, own_share * head + (1.0 - own_share) * aligned.astype(jnp.float32), head
    )
    blended = jnp.concatenate([mixed.astype(jnp.bfloat16), decoded[OVMAX:]], axis=0)
    return blended[None]


def solution(mesh):
    in_specs = (
        P("tile", None, None, "col", None),
        P("tile"),
        P(),
        P(),
        P(None, None, None, "col", None),
        P(),
        P(),
        P(None, None, None, "col", None),
        P(),
    )
    out_specs = P("tile", None, None, "col", None)
    return jax.shard_map(shards, mesh=mesh, in_specs=in_specs, out_specs=out_specs, check_vma=False)
```

profile of v0, /device:TPU:64, one launch (start us, length us, event | category | flops | bytes accessed | tf_op | source)
XLA Modules:
  0.0 126.9 jit_solution(7533719370882032942)
XLA Ops:
  6.5 0.7 all-gather.3.cloned.1.call-update
  7.3 1.0 convert_reduce_fusion
  8.3 1.0 fusion.7
  9.8 0.6 broadcast_in_dim.51
  10.4 5.4 %all-to-all-start = ((f32[16,1,64]{2,1,0:T(1,128)}), f32[16,1,64]{2,1,0:T(1,128)S(1)}, u32[]{:S(2)}, u32[]{:S(2)}) async-start(f32[16,1,64]{2,1,0:T(1,128)} %broadcast_in_dim.51), calls=%async_computation | async-start | bytes 16384 | tf_op jit(solution)/shard_map/all_to_all | solution.py:13
  15.9 0.7 all-gather.5.cloned.1.call-update
  17.2 4.6 %all-to-all-done = f32[16,1,64]{2,1,0:T(1,128)S(1)} async-done(((f32[16,1,64]{2,1,0:T(1,128)}), f32[16,1,64]{2,1,0:T(1,128)S(1)}, u32[]{:S(2)}, u32[]{:S(2)}) %all-to-all-start) | async-done | bytes 4128 | tf_op jit(solution)/shard_map/all_to_all | solution.py:13
  22.3 1.1 fusion.12
  23.5 1.8 %collective-permute-start = (bf16[17,4,2,256]{3,2,1,0:T(2,128)(2,1)S(1)}, bf16[17,4,2,256]{3,2,1,0:T(2,128)(2,1)S(1)}, u32[]{:S(2)}, u32[]{:S(2)}) collective-permute-start(bf16[17,4,2,256]{3,2,1,0:T(2,128)(2,1)S(1)} %get-tuple-element.61), channel_id=1, source_target_pairs={{0,1},{1,2},{2,3},{3,4},{4,5},{5,6},{6,7},{7,8},{8,9},{9,10},{10,1... | collective-permute-start | bytes 208904 | tf_op jit(solution)/shard_map/ppermute | solution.py:36
  25.3 1.3 %collective-permute-start.1 = (bf16[17,4,2,256]{3,2,1,0:T(2,128)(2,1)S(1)}, bf16[17,4,2,256]{3,2,1,0:T(2,128)(2,1)S(1)}, u32[]{:S(2)}, u32[]{:S(2)}) collective-permute-start(bf16[17,4,2,256]{3,2,1,0:T(2,128)(2,1)S(1)} %get-tuple-element.62), channel_id=1, source_target_pairs={{1,0},{2,1},{3,2},{4,3},{5,4},{6,5},{7,6},{8,7},{9,8},{10,9},{11,1... | collective-permute-start | bytes 208904 | tf_op jit(solution)/shard_map/ppermute | solution.py:37
  26.6 0.5 convert_divide_fusion
  27.1 1.7 %collective-permute-done.1 = bf16[17,4,2,256]{3,2,1,0:T(2,128)(2,1)S(1)} collective-permute-done((bf16[17,4,2,256]{3,2,1,0:T(2,128)(2,1)S(1)}, bf16[17,4,2,256]{3,2,1,0:T(2,128)(2,1)S(1)}, u32[]{:S(2)}, u32[]{:S(2)}) %collective-permute-start.1) | collective-permute-done | bytes 69664 | tf_op jit(solution)/shard_map/ppermute | solution.py:37
  28.8 0.2 pad_maximum_fusion
  29.0 0.4 copy-done.18
  29.4 2.0 %pad_slice_fusion.24 = (bf16[17,4,6,256]{3,2,1,0:T(8,128)(2,1)S(1)}, bf16[17,4,6,256]{3,2,1,0:T(8,128)(2,1)}, bf16[17,4,6,256]{3,2,1,0:T(8,128)(2,1)}, bf16[17,4...) fusion(bf16[17,4,8,256]{3,2,1,0:T(8,128)(2,1)S(1)} %pad_maximum, ...), kind=kLoop, calls=%fused_computation.24 | loop fusion | bytes 4247552 | tf_op jit(solution)/shard_map/slice | solution.py:59
  31.4 0.3 pad_slice_fusion.25
  31.7 1.7 %reshape.223 = bf16[408,256]{1,0:T(8,128)(2,1)} reshape(bf16[17,4,6,256]{3,2,1,0:T(8,128)(2,1)} %get-tuple-element.35) | data formatting | bytes 417792 | tf_op jit(solution)/shard_map/reshape | solution.py:63
  33.5 0.8 reshape.222
  34.2 1.7 %reshape.224 = bf16[408,256]{1,0:T(8,128)(2,1)} reshape(bf16[17,4,6,256]{3,2,1,0:T(8,128)(2,1)} %get-tuple-element.36) | data formatting | bytes 417792 | tf_op jit(solution)/shard_map/reshape | solution.py:63
  36.0 1.7 %reshape.225 = bf16[408,256]{1,0:T(8,128)(2,1)} reshape(bf16[17,4,6,256]{3,2,1,0:T(8,128)(2,1)} %get-tuple-element.37) | data formatting | bytes 417792 | tf_op jit(solution)/shard_map/reshape | solution.py:63
  37.7 1.7 %reshape.226 = bf16[408,256]{1,0:T(8,128)(2,1)} reshape(bf16[17,4,6,256]{3,2,1,0:T(8,128)(2,1)} %get-tuple-element.38) | data formatting | bytes 417792 | tf_op jit(solution)/shard_map/reshape | solution.py:63
  39.4 1.7 %reshape.227 = bf16[408,256]{1,0:T(8,128)(2,1)} reshape(bf16[17,4,6,256]{3,2,1,0:T(8,128)(2,1)} %get-tuple-element.39) | data formatting | bytes 417792 | tf_op jit(solution)/shard_map/reshape | solution.py:63
  41.1 1.7 %reshape.228 = bf16[408,256]{1,0:T(8,128)(2,1)} reshape(bf16[17,4,6,256]{3,2,1,0:T(8,128)(2,1)} %get-tuple-element.40) | data formatting | bytes 417792 | tf_op jit(solution)/shard_map/reshape | solution.py:63
  42.8 1.7 %reshape.229 = bf16[408,256]{1,0:T(8,128)(2,1)} reshape(bf16[17,4,6,256]{3,2,1,0:T(8,128)(2,1)} %get-tuple-element.41) | data formatting | bytes 417792 | tf_op jit(solution)/shard_map/reshape | solution.py:63
  44.6 1.7 %reshape.230 = bf16[408,256]{1,0:T(8,128)(2,1)} reshape(bf16[17,4,6,256]{3,2,1,0:T(8,128)(2,1)} %get-tuple-element.42) | data formatting | bytes 417792 | tf_op jit(solution)/shard_map/reshape | solution.py:63
  46.3 1.7 %reshape.231 = bf16[408,256]{1,0:T(8,128)(2,1)} reshape(bf16[17,4,6,256]{3,2,1,0:T(8,128)(2,1)} %get-tuple-element.43) | data formatting | bytes 417792 | tf_op jit(solution)/shard_map/reshape | solution.py:63
  48.0 1.7 %reshape.232 = bf16[408,256]{1,0:T(8,128)(2,1)} reshape(bf16[17,4,6,256]{3,2,1,0:T(8,128)(2,1)} %get-tuple-element.44) | data formatting | bytes 417792 | tf_op jit(solution)/shard_map/reshape | solution.py:63
  49.7 1.7 %reshape.233 = bf16[408,256]{1,0:T(8,128)(2,1)} reshape(bf16[17,4,6,256]{3,2,1,0:T(8,128)(2,1)} %get-tuple-element.45) | data formatting | bytes 417792 | tf_op jit(solution)/shard_map/reshape | solution.py:63
  51.5 1.7 %reshape.234 = bf16[408,256]{1,0:T(8,128)(2,1)} reshape(bf16[17,4,6,256]{3,2,1,0:T(8,128)(2,1)} %get-tuple-element.46) | data formatting | bytes 417792 | tf_op jit(solution)/shard_map/reshape | solution.py:63
  53.2 0.7 reshape.235
  54.5 0.7 reshape.244
  55.3 0.3 pad_maximum_fusion.2
  55.5 0.8 reshape.243
  56.3 0.8 reshape.246
  57.3 1.4 %fusion.17 = f32[408,256]{1,0:T(8,128)S(1)} fusion(bf16[408,256]{1,0:T(8,128)(2,1)} %reshape.223, bf16[3,3,3,256,256]{4,3,2,1,0:T(8,128)(2,1)} %all-gather.3.cloned.1.call-done), kind=kOutput, calls=%fused_computation.178 | convolution fusion | flops 53477376 | bytes 757760 | tf_op jit(solution)/shard_map/dot_general | solution.py:62
  58.7 1.3 fusion.16
  60.0 1.2 convolution_add_fusion.23
  61.2 1.3 convolution_add_fusion.22
  62.5 1.2 convolution_add_fusion.21
  65.2 0.2 convolution_add_fusion.15
  66.9 0.2 convolution_add_fusion.8
  68.0 0.2 fusion
  68.3 0.2 fusion.1
  68.8 0.2 fusion.3
  69.7 0.6 broadcast_in_dim.54
  70.3 8.9 %all-to-all-start.1 = ((f32[16,1,64]{2,1,0:T(1,128)}), f32[16,1,64]{2,1,0:T(1,128)S(1)}, u32[]{:S(2)}, u32[]{:S(2)}) async-start(f32[16,1,64]{2,1,0:T(1,128)} %broadcast_in_dim.54), calls=%async_computation.1 | async-start | bytes 16384 | tf_op jit(solution)/shard_map/all_to_all | solution.py:13
  79.2 6.0 %all-to-all-done.1 = f32[16,1,64]{2,1,0:T(1,128)S(1)} async-done(((f32[16,1,64]{2,1,0:T(1,128)}), f32[16,1,64]{2,1,0:T(1,128)S(1)}, u32[]{:S(2)}, u32[]{:S(2)}) %all-to-all-start.1) | async-done | bytes 4128 | tf_op jit(solution)/shard_map/all_to_all | solution.py:13
  85.9 0.8 pad_slice_fusion
  86.7 1.2 pad_slice_fusion.1
  87.9 0.7 reshape.251
  88.6 0.7 reshape.253
  89.3 0.7 reshape.254
  90.7 0.9 reshape.270
  91.6 0.9 reshape.271
  92.7 0.9 reshape.274
  93.7 5.8 %all-gather.5.cloned.1.call-done = bf16[3,3,3,256,256]{4,3,2,1,0:T(8,128)(2,1)} async-done(((bf16[3,3,3,16,256]{4,3,2,1,0:T(8,128)(2,1)}), bf16[3,3,3,256,256]{4,3,2,1,0:T(8,128)(2,1)}) %all-gather.5.cloned.1.call-update) | async-done | bytes 3538960 | tf_op jit(solution)/shard_map/all_gather | solution.py:106
  99.5 1.3 %fusion.14 = f32[272,256]{1,0:T(8,128)S(1)} fusion(bf16[272,256]{1,0:T(8,128)(2,1)} %reshape.251, bf16[3,3,3,256,256]{4,3,2,1,0:T(8,128)(2,1)} %all-gather.5.cloned.1.call-done), kind=kOutput, calls=%fused_computation.149 | convolution fusion | flops 35651584 | bytes 548864 | tf_op jit(solution)/shard_map/dot_general | solution.py:62
  100.8 1.1 convolution_add_fusion.49
  101.9 1.2 convolution_add_fusion.48
  103.1 1.2 convolution_add_fusion.47
  104.3 1.1 convolution_add_fusion.46
  110.0 4.3 %collective-permute-start.2 = (bf16[4,4,4,256]{3,2,1,0:T(4,128)(2,1)S(1)}, bf16[4,4,4,256]{3,2,1,0:T(4,128)(2,1)S(1)}, u32[]{:S(2)}, u32[]{:S(2)}) collective-permute-start(bf16[4,4,4,256]{3,2,1,0:T(4,128)(2,1)S(1)} %slice.536), channel_id=1, source_target_pairs={{0,16},{16,32},{32,48},{48,64},{64,80},{80,96},{96,112},{112,128},... | collective-permute-start | bytes 98312 | tf_op jit(solution)/shard_map/ppermute | solution.py:45
  114.4 4.8 %collective-permute-done.2 = bf16[4,4,4,256]{3,2,1,0:T(4,128)(2,1)S(1)} collective-permute-done((bf16[4,4,4,256]{3,2,1,0:T(4,128)(2,1)S(1)}, bf16[4,4,4,256]{3,2,1,0:T(4,128)(2,1)S(1)}, u32[]{:S(2)}, u32[]{:S(2)}) %collective-permute-start.2) | collective-permute-done | bytes 32800 | tf_op jit(solution)/shard_map/ppermute | solution.py:45
  119.3 0.8 maximum_bitcast_fusion
  (154 shorter events, 12.4 us)
Async XLA Ops:
  6.5 50.8 %all-gather.3.cloned.1.call-start = ((), (), s32[]{:S(2)}) async-start(), calls=%async_computation.2 | async-start | bytes 3760128 | tf_op jit(solution)/shard_map/all_gather | solution.py:105
  10.4 11.4 %all-to-all-start = ((f32[16,1,64]{2,1,0:T(1,128)}), f32[16,1,64]{2,1,0:T(1,128)S(1)}, u32[]{:S(2)}, u32[]{:S(2)}) async-start(f32[16,1,64]{2,1,0:T(1,128)} %broadcast_in_dim.51), calls=%async_computation | async-start | bytes 16384 | tf_op jit(solution)/shard_map/all_to_all | solution.py:13
  15.8 83.7 %all-gather.5.cloned.1.call-start = ((), (), s32[]{:S(2)}) async-start(), calls=%async_computation.3 | async-start | bytes 3760128 | tf_op jit(solution)/shard_map/all_gather | solution.py:106
  23.5 3.6 %collective-permute-start = (bf16[17,4,2,256]{3,2,1,0:T(2,128)(2,1)S(1)}, bf16[17,4,2,256]{3,2,1,0:T(2,128)(2,1)S(1)}, u32[]{:S(2)}, u32[]{:S(2)}) collective-permute-start(bf16[17,4,2,256]{3,2,1,0:T(2,128)(2,1)S(1)} %get-tuple-element.61), channel_id=1, source_target_pairs={{0,1},{1,2},{2,3},{3,4},{4,5},{5,6},{6,7},{7,8},{8,9},{9,10},{10,1... | collective-permute-start | bytes 208904 | tf_op jit(solution)/shard_map/ppermute | solution.py:36
  25.3 3.5 %collective-permute-start.1 = (bf16[17,4,2,256]{3,2,1,0:T(2,128)(2,1)S(1)}, bf16[17,4,2,256]{3,2,1,0:T(2,128)(2,1)S(1)}, u32[]{:S(2)}, u32[]{:S(2)}) collective-permute-start(bf16[17,4,2,256]{3,2,1,0:T(2,128)(2,1)S(1)} %get-tuple-element.62), channel_id=1, source_target_pairs={{1,0},{2,1},{3,2},{4,3},{5,4},{6,5},{7,6},{8,7},{9,8},{10,9},{11,1... | collective-permute-start | bytes 208904 | tf_op jit(solution)/shard_map/ppermute | solution.py:37
  28.8 0.6 copy-start.18
  34.2 18.9 %copy-start.3 = (bf16[17,4,6,256]{3,2,1,0:T(8,128)(2,1)S(1)}, bf16[17,4,6,256]{3,2,1,0:T(8,128)(2,1)}, u32[]{:S(2)}) copy-start(bf16[17,4,6,256]{3,2,1,0:T(8,128)(2,1)} %get-tuple-element.47) | copy-start | bytes 626692
  53.9 1.3 %copy-start.19 = (bf16[17,4,2,256]{3,2,1,0:T(2,128)(2,1)S(1)}, bf16[17,4,2,256]{3,2,1,0:T(2,128)(2,1)}, u32[]{:S(2)}) copy-start(bf16[17,4,2,256]{3,2,1,0:T(2,128)(2,1)} %copy-done.18) | copy-start | bytes 208900
  57.1 6.9 %copy-start.14 = (bf16[408,256]{1,0:T(8,128)(2,1)S(1)}, bf16[408,256]{1,0:T(8,128)(2,1)}, u32[]{:S(2)}) copy-start(bf16[408,256]{1,0:T(8,128)(2,1)} %reshape.226) | copy-start | bytes 626692
  57.3 6.9 %copy-start.13 = (bf16[408,256]{1,0:T(8,128)(2,1)S(1)}, bf16[408,256]{1,0:T(8,128)(2,1)}, u32[]{:S(2)}) copy-start(bf16[408,256]{1,0:T(8,128)(2,1)} %reshape.227) | copy-start | bytes 626692
  57.3 5.2 %copy-start.1 = (bf16[3,3,3,256,256]{4,3,2,1,0:T(8,128)(2,1)S(1)}, bf16[3,3,3,256,256]{4,3,2,1,0:T(8,128)(2,1)}, u32[]{:S(2)}) copy-start(bf16[3,3,3,256,256]{4,3,2,1,0:T(8,128)(2,1)} %all-gather.3.cloned.1.call-done) | copy-start | bytes 10616836
  57.3 6.4 %copy-start.15 = (bf16[408,256]{1,0:T(8,128)(2,1)S(1)}, bf16[408,256]{1,0:T(8,128)(2,1)}, u32[]{:S(2)}) copy-start(bf16[408,256]{1,0:T(8,128)(2,1)} %reshape.246) | copy-start | bytes 626692
  58.7 5.7 %copy-start.12 = (bf16[408,256]{1,0:T(8,128)(2,1)S(1)}, bf16[408,256]{1,0:T(8,128)(2,1)}, u32[]{:S(2)}) copy-start(bf16[408,256]{1,0:T(8,128)(2,1)} %reshape.228) | copy-start | bytes 626692
  61.2 3.5 %copy-start.11 = (bf16[408,256]{1,0:T(8,128)(2,1)S(1)}, bf16[408,256]{1,0:T(8,128)(2,1)}, u32[]{:S(2)}) copy-start(bf16[408,256]{1,0:T(8,128)(2,1)} %reshape.229) | copy-start | bytes 626692
  62.5 2.4 %copy-start.10 = (bf16[408,256]{1,0:T(8,128)(2,1)S(1)}, bf16[408,256]{1,0:T(8,128)(2,1)}, u32[]{:S(2)}) copy-start(bf16[408,256]{1,0:T(8,128)(2,1)} %reshape.230) | copy-start | bytes 626692
  63.7 1.5 %copy-start.9 = (bf16[408,256]{1,0:T(8,128)(2,1)S(1)}, bf16[408,256]{1,0:T(8,128)(2,1)}, u32[]{:S(2)}) copy-start(bf16[408,256]{1,0:T(8,128)(2,1)} %reshape.231) | copy-start | bytes 626692
  64.0 1.5 %copy-start.8 = (bf16[408,256]{1,0:T(8,128)(2,1)S(1)}, bf16[408,256]{1,0:T(8,128)(2,1)}, u32[]{:S(2)}) copy-start(bf16[408,256]{1,0:T(8,128)(2,1)} %reshape.232) | copy-start | bytes 626692
  64.2 1.5 %copy-start.7 = (bf16[408,256]{1,0:T(8,128)(2,1)S(1)}, bf16[408,256]{1,0:T(8,128)(2,1)}, u32[]{:S(2)}) copy-start(bf16[408,256]{1,0:T(8,128)(2,1)} %reshape.233) | copy-start | bytes 626692
  64.5 1.4 %copy-start.6 = (bf16[408,256]{1,0:T(8,128)(2,1)S(1)}, bf16[408,256]{1,0:T(8,128)(2,1)}, u32[]{:S(2)}) copy-start(bf16[408,256]{1,0:T(8,128)(2,1)} %reshape.234) | copy-start | bytes 626692
  64.7 1.4 %copy-start.4 = (bf16[408,256]{1,0:T(8,128)(2,1)S(1)}, bf16[408,256]{1,0:T(8,128)(2,1)}, u32[]{:S(2)}) copy-start(bf16[408,256]{1,0:T(8,128)(2,1)} %reshape.235) | copy-start | bytes 626692
  66.6 1.4 %copy-start.5 = (bf16[408,256]{1,0:T(8,128)(2,1)S(1)}, bf16[408,256]{1,0:T(8,128)(2,1)}, u32[]{:S(2)}) copy-start(bf16[408,256]{1,0:T(8,128)(2,1)} %reshape.243) | copy-start | bytes 626692
  68.0 17.6 %copy-start.20 = (f32[256]{0:T(256)S(1)}, f32[256]{0:T(256)}, u32[]{:S(2)}) copy-start(f32[256]{0:T(256)} %param.15) | copy-start | bytes 3076
  68.0 17.6 %copy-start.21 = (f32[256]{0:T(256)S(1)}, f32[256]{0:T(256)}, u32[]{:S(2)}) copy-start(f32[256]{0:T(256)} %param.14) | copy-start | bytes 3076
  70.3 14.9 %all-to-all-start.1 = ((f32[16,1,64]{2,1,0:T(1,128)}), f32[16,1,64]{2,1,0:T(1,128)S(1)}, u32[]{:S(2)}, u32[]{:S(2)}) async-start(f32[16,1,64]{2,1,0:T(1,128)} %broadcast_in_dim.54), calls=%async_computation.1 | async-start | bytes 16384 | tf_op jit(solution)/shard_map/all_to_all | solution.py:13
  87.9 4.6 %copy-start.17 = (bf16[17,4,4,256]{3,2,1,0:T(4,128)(2,1)S(1)}, bf16[17,4,4,256]{3,2,1,0:T(4,128)(2,1)}, u32[]{:S(2)}) copy-start(bf16[17,4,4,256]{3,2,1,0:T(4,128)(2,1)} %get-tuple-element.32) | copy-start | bytes 417796
  87.9 4.7 %copy-start.16 = (bf16[17,4,4,256]{3,2,1,0:T(4,128)(2,1)S(1)}, bf16[17,4,4,256]{3,2,1,0:T(4,128)(2,1)}, u32[]{:S(2)}) copy-start(bf16[17,4,4,256]{3,2,1,0:T(4,128)(2,1)} %get-tuple-element.31) | copy-start | bytes 417796
  99.5 5.9 %copy-start = (bf16[3,3,3,256,256]{4,3,2,1,0:T(8,128)(2,1)S(1)}, bf16[3,3,3,256,256]{4,3,2,1,0:T(8,128)(2,1)}, u32[]{:S(2)}) copy-start(bf16[3,3,3,256,256]{4,3,2,1,0:T(8,128)(2,1)} %all-gather.5.cloned.1.call-done) | copy-start | bytes 10616836
  108.2 1.7 %copy-start.2 = (bf16[1,17,4,4,256]{4,3,2,1,0:T(4,128)(2,1)S(1)}, bf16[1,17,4,4,256]{4,3,2,1,0:T(4,128)(2,1)}, u32[]{:S(2)}) copy-start(bf16[1,17,4,4,256]{4,3,2,1,0:T(4,128)(2,1)} %param.9) | copy-start | bytes 417796
  108.2 1.7 %copy-start.22 = (f32[256]{0:T(256)S(1)}, f32[256]{0:T(256)}, u32[]{:S(2)}) copy-start(f32[256]{0:T(256)} %param.17) | copy-start | bytes 3076
  108.4 10.8 %copy-start.23 = (f32[4]{0:T(128)S(1)}, f32[4]{0:T(128)}, u32[]{:S(2)}) copy-start(f32[4]{0:T(128)} %get-tuple-element.68) | copy-start | bytes 52
  110.0 9.2 %collective-permute-start.2 = (bf16[4,4,4,256]{3,2,1,0:T(4,128)(2,1)S(1)}, bf16[4,4,4,256]{3,2,1,0:T(4,128)(2,1)S(1)}, u32[]{:S(2)}, u32[]{:S(2)}) collective-permute-start(bf16[4,4,4,256]{3,2,1,0:T(4,128)(2,1)S(1)} %slice.536), channel_id=1, source_target_pairs={{0,16},{16,32},{32,48},{48,64},{64,80},{80,96},{96,112},{112,128},... | collective-permute-start | bytes 98312 | tf_op jit(solution)/shard_map/ppermute | solution.py:45
Sparse Core Ops, SparseCore 0:
  9.4 46.1 all-gather.2
  57.7 41.7 all-gather.4
where the time goes:
time: 128 us; the launch traced here: 127 us
  local copies, waits for them, and re-layouts  38.3 us (30%)
  waiting for transfers between devices  24.2 us (19%)
  starting transfers between devices  21.7 us (17%)
  matrix products  21.3 us (17%)
  between operations  15.1 us (12%)
  other arithmetic  6.35 us (5%)
    reshape x54, local copies, waits for them, and re-layouts, conv_taps(): window.reshape(-1, channels)  31 us
    dot_general x54, matrix products, conv_taps(): jnp.dot(window.reshape(-1, channels), kernel[tap_t, tap_h, tap_w], prefer...  21.3 us
    all_to_all x2, starting transfers between devices, copy_for_each(): return lax.all_to_all(copies, axis, split_axis=0, concat_axis=0, tiled=True)  14.3 us
    all_to_all x2, waiting for transfers between devices, copy_for_each(): return lax.all_to_all(copies, axis, split_axis=0, concat_axis=0, tiled=True)  10.6 us
    all_gather x1, waiting for transfers between devices, shards(): lax.all_gather(weight_two, 'col', axis=3, tiled=True)  5.76 us
    ppermute x1, waiting for transfers between devices, shifted(): return lax.ppermute(block, axis, route)  4.79 us
    slice x4, local copies, waits for them, and re-layouts, conv_taps(): padded[tap_t:tap_t + frames, tap_h:tap_h + height, tap_w:tap_w + out_width]  4.33 us
    ppermute x1, starting transfers between devices, shifted(): return lax.ppermute(block, axis, route)  4.3 us
  transfers between devices with their start and end apart: 7, of which 5 were waited for; matrix products, arithmetic and copies ran while one was open for 43% of the time, Pallas kernels for 0%

commit v1 on v0

--- a/solution.py
+++ b/solution.py
@@ -103,7 +103,9 @@
     act_one = norm_silu(latent_full, latent_full, norm_gain_one, norm_shift_one)
     kernel_one, kernel_two = (
         lax.all_gather(weight_one, "col", axis=3, tiled=True),
-        lax.all_gather(weight_two, "col", axis=3, tiled=True),
+        jnp.concatenate(
+            lax.all_to_all(jnp.stack([weight_two] * lax.axis_size("col")), "col", 0, 0), axis=3
+        ),
     )
     margin = extended_2(act_one, (("col", 2),), 2)
     hidden = conv_taps(margin, kernel=kernel_one).astype(jnp.bfloat16)

time: 128 us -> 260 us (2.03)
  local copies, waits for them, and re-layouts: 38.3 us -> 115 us
  starting transfers between devices: 21.7 us -> 72.8 us
  other arithmetic: 6.35 us -> 15.2 us
  waiting for transfers between devices: 24.2 us -> 16.3 us
    reshape x54, local copies, waits for them, and re-layouts: 31 us -> 89.6 us  [conv_taps(): window.reshape(-1, channels)]
    all_to_all x2, starting transfers between devices: 14.3 us -> 61.7 us  [copy_for_each(): return lax.all_to_all(copies, axis, split_axis=0, concat_axis=0, tiled=True)]
    all_gather x1 -> x0, waiting for transfers between devices: 5.76 us -> none  [shards(): lax.all_gather(weight_two, 'col', axis=3, tiled=True)]
    slice x4, local copies, waits for them, and re-layouts: 4.33 us -> 8.85 us  [conv_taps(): padded[tap_t:tap_t + frames, tap_h:tap_h + height, tap_w:tap_w + out_width]]
    all_to_all x0 -> x1, starting transfers between devices: none -> 3.75 us  [shards(): lax.all_to_all(jnp.stack([weight_two] * lax.axis_size('col')), 'col', 0, 0)]
    another operation x0 -> x1, local copies, waits for them, and re-layouts: none -> 2.9 us  [shards(): jnp.stack([weight_two] * lax.axis_size('col'))]
    reduce_sum x7, other arithmetic: 2.66 us -> 5.41 us  [group_total(): jnp.sum(values, axis=(0, 1, 2)).reshape(GROUPS, per_group).sum(axis=1)]
  transfers between devices with their start and end apart: 7 -> 7, of which waited for: 5 -> 4; matrix products, arithmetic and copies ran while one was open for 43% -> 34% of each run, Pallas kernels for 0% -> 0%
where the time goes in v1:
time: 260 us; the launch traced here: 258 us
  local copies, waits for them, and re-layouts  115 us (44%)
  starting transfers between devices  72.8 us (28%)
  matrix products  22.7 us (9%)
  waiting for transfers between devices  16.3 us (6%)
  between operations  15.3 us (6%)
  other arithmetic  15.2 us (6%)
    reshape x54, local copies, waits for them, and re-layouts, conv_taps(): window.reshape(-1, channels)  89.6 us
    all_to_all x2, starting transfers between devices, copy_for_each(): return lax.all_to_all(copies, axis, split_axis=0, concat_axis=0, tiled=True)  61.7 us
    dot_general x54, matrix products, conv_taps(): jnp.dot(window.reshape(-1, channels), kernel[tap_t, tap_h, tap_w], prefer...  22.7 us
    slice x4, local copies, waits for them, and re-layouts, conv_taps(): padded[tap_t:tap_t + frames, tap_h:tap_h + height, tap_w:tap_w + out_width]  8.85 us
    all_to_all x2, waiting for transfers between devices, copy_for_each(): return lax.all_to_all(copies, axis, split_axis=0, concat_axis=0, tiled=True)  8.3 us
    reduce_sum x7, other arithmetic, group_total(): jnp.sum(values, axis=(0, 1, 2)).reshape(GROUPS, per_group).sum(axis=1)  5.41 us
  transfers between devices with their start and end apart: 7, of which 4 were waited for; matrix products, arithmetic and copies ran while one was open for 34% of the time, Pallas kernels for 0%

profile of v1, /device:TPU:64, one launch (start us, length us, event | category | flops | bytes accessed | tf_op | source)
XLA Modules:
  0.0 257.8 jit_solution(8607466924679936408)
XLA Ops:
  10.4 5.4 %all-to-all-start = ((f32[16,1,64]{2,1,0:T(1,128)}), f32[16,1,64]{2,1,0:T(1,128)S(1)}, u32[]{:S(2)}, u32[]{:S(2)}) async-start(f32[16,1,64]{2,1,0:T(1,128)} %broadcast_in_dim.51), calls=%async_computation | async-start | bytes 16384 | tf_op jit(solution)/shard_map/all_to_all | solution.py:13
  16.5 5.3 %all-to-all-done = f32[16,1,64]{2,1,0:T(1,128)S(1)} async-done(((f32[16,1,64]{2,1,0:T(1,128)}), f32[16,1,64]{2,1,0:T(1,128)S(1)}, u32[]{:S(2)}, u32[]{:S(2)}) %all-to-all-start) | async-done | bytes 4128 | tf_op jit(solution)/shard_map/all_to_all | solution.py:13
  21.8 2.9 %stack.2 = bf16[16,3,3,3,16,256]{5,4,3,2,1,0:T(8,128)(2,1)} broadcast(bf16[3,3,3,16,256]{4,3,2,1,0:T(8,128)(2,1)} %param.16), dimensions={1,2,3,4,5} | broadcast | bytes 3760128 | tf_op jit(solution)/shard_map/stack | solution.py:107
  24.7 3.8 %all-to-all-start.2 = ((bf16[16,3,3,3,16,256]{5,4,3,2,1,0:T(8,128)(2,1)}), bf16[16,3,3,3,16,256]{5,4,3,2,1,0:T(8,128)(2,1)S(1)}, u32[]{:S(2)}, u32[]{:S(2)}) async-start(bf16[16,3,3,3,16,256]{5,4,3,2,1,0:T(8,128)(2,1)} %stack.2), calls=%async_computation.2 | async-start | bytes 7077888 | tf_op jit(solution)/shard_map/all_to_all | solution.py:107
  32.4 2.2 collective-permute-start
  36.4 2.5 collective-permute-done.1
  40.4 2.5 pad_slice_fusion.24
  43.0 1.7 reshape.231
  44.7 2.9 %pad_slice_fusion.25 = (bf16[17,4,6,256]{3,2,1,0:T(8,128)(2,1)}, bf16[17,4,6,256]{3,2,1,0:T(8,128)(2,1)}, bf16[17,4,6,256]{3,2,1,0:T(8,128)(2,1)}, bf16[17,4,6,2...) fusion(bf16[17,4,8,256]{3,2,1,0:T(8,128)(2,1)} %copy-done.1), kind=kLoop, calls=%fused_computation.25 | loop fusion | bytes 1810432 | tf_op jit(solution)/shard_map/slice | solution.py:59
  47.6 1.7 reshape.230
  49.3 1.7 reshape.232
  51.0 1.7 reshape.233
  52.7 1.7 reshape.234
  54.4 1.7 reshape.235
  56.1 1.7 reshape.236
  57.8 1.7 reshape.237
  59.5 1.7 reshape.238
  61.3 1.7 reshape.239
  63.0 1.7 reshape.240
  64.7 1.7 reshape.241
  66.4 1.7 reshape.242
  68.1 1.7 reshape.243
  69.8 1.7 reshape.244
  71.5 1.7 reshape.245
  73.2 1.7 reshape.246
  74.9 1.7 reshape.247
  76.7 1.7 reshape.248
  78.4 1.7 reshape.249
  80.1 1.7 reshape.250
  81.8 1.7 reshape.252
  83.5 2.2 pad_maximum_fusion.2
  85.7 1.7 reshape.251
  87.5 1.7 reshape.254
  89.2 1.7 reshape.253
  90.9 1.7 reshape.255
  92.6 1.7 reshape.256
  107.0 1.9 reshape.289
  108.8 1.8 slice_reduce_fusion
  114.9 56.2 %all-to-all-start.1 = ((f32[16,1,64]{2,1,0:T(1,128)}), f32[16,1,64]{2,1,0:T(1,128)S(1)}, u32[]{:S(2)}, u32[]{:S(2)}) async-start(f32[16,1,64]{2,1,0:T(1,128)} %broadcast_in_dim.54), calls=%async_computation.1 | async-start | bytes 16384 | tf_op jit(solution)/shard_map/all_to_all | solution.py:13
  171.7 2.4 copy.14
  174.2 2.9 %all-to-all-done.1 = f32[16,1,64]{2,1,0:T(1,128)S(1)} async-done(((f32[16,1,64]{2,1,0:T(1,128)}), f32[16,1,64]{2,1,0:T(1,128)S(1)}, u32[]{:S(2)}, u32[]{:S(2)}) %all-to-all-start.1) | async-done | bytes 4128 | tf_op jit(solution)/shard_map/all_to_all | solution.py:13
  182.4 2.2 pad_slice_fusion
  184.6 1.6 reshape.259
  186.2 1.6 reshape.262
  187.8 1.6 reshape.263
  189.4 1.6 reshape.264
  192.6 1.6 reshape.266
  194.2 1.6 reshape.267
  199.0 1.6 reshape.270
  200.6 1.6 reshape.271
  202.2 1.6 reshape.272
  207.1 1.6 reshape.275
  208.7 1.6 reshape.276
  210.3 1.6 reshape.277
  213.5 1.6 reshape.279
  215.1 1.6 reshape.280
  218.3 1.6 reshape.282
  219.9 1.6 reshape.283
  221.5 1.6 reshape.284
  223.1 1.6 reshape.285
  224.7 1.6 reshape.286
  226.3 1.6 reshape.287
  241.2 3.9 %collective-permute-start.2 = (bf16[4,4,4,256]{3,2,1,0:T(4,128)(2,1)S(1)}, bf16[4,4,4,256]{3,2,1,0:T(4,128)(2,1)S(1)}, u32[]{:S(2)}, u32[]{:S(2)}) collective-permute-start(bf16[4,4,4,256]{3,2,1,0:T(4,128)(2,1)S(1)} %slice.536), channel_id=1, source_target_pairs={{0,16},{16,32},{32,48},{48,64},{64,80},{80,96},{96,112},{112,128},... | collective-permute-start | bytes 98312 | tf_op jit(solution)/shard_map/ppermute | solution.py:45
  245.2 4.8 %collective-permute-done.2 = bf16[4,4,4,256]{3,2,1,0:T(4,128)(2,1)S(1)} collective-permute-done((bf16[4,4,4,256]{3,2,1,0:T(4,128)(2,1)S(1)}, bf16[4,4,4,256]{3,2,1,0:T(4,128)(2,1)S(1)}, u32[]{:S(2)}, u32[]{:S(2)}) %collective-permute-start.2) | collective-permute-done | bytes 32800 | tf_op jit(solution)/shard_map/ppermute | solution.py:45
  (213 shorter events, 58.2 us)
Async XLA Ops:
  6.5 87.8 %all-gather.2.cloned.1.call-start = ((), (), s32[]{:S(2)}) async-start(), calls=%async_computation.3 | async-start | bytes 3760128 | tf_op jit(solution)/shard_map/all_gather | solution.py:105
  10.4 11.4 %all-to-all-start = ((f32[16,1,64]{2,1,0:T(1,128)}), f32[16,1,64]{2,1,0:T(1,128)S(1)}, u32[]{:S(2)}, u32[]{:S(2)}) async-start(f32[16,1,64]{2,1,0:T(1,128)} %broadcast_in_dim.51), calls=%async_computation | async-start | bytes 16384 | tf_op jit(solution)/shard_map/all_to_all | solution.py:13
  24.7 89.5 %all-to-all-start.2 = ((bf16[16,3,3,3,16,256]{5,4,3,2,1,0:T(8,128)(2,1)}), bf16[16,3,3,3,16,256]{5,4,3,2,1,0:T(8,128)(2,1)S(1)}, u32[]{:S(2)}, u32[]{:S(2)}) async-start(bf16[16,3,3,3,16,256]{5,4,3,2,1,0:T(8,128)(2,1)} %stack.2), calls=%async_computation.2 | async-start | bytes 7077888 | tf_op jit(solution)/shard_map/all_to_all | solution.py:107
  32.3 6.6 %copy-start.3 = (bf16[17,4,4,256]{3,2,1,0:T(4,128)(2,1)}, bf16[17,4,4,256]{3,2,1,0:T(4,128)(2,1)S(1)}, u32[]{:S(2)}) copy-start(bf16[17,4,4,256]{3,2,1,0:T(4,128)(2,1)S(1)} %fusion.12) | copy-start | bytes 417796
  32.4 4.0 %collective-permute-start = (bf16[17,4,2,256]{3,2,1,0:T(2,128)(2,1)S(1)}, bf16[17,4,2,256]{3,2,1,0:T(2,128)(2,1)S(1)}, u32[]{:S(2)}, u32[]{:S(2)}) collective-permute-start(bf16[17,4,2,256]{3,2,1,0:T(2,128)(2,1)S(1)} %get-tuple-element.61), channel_id=1, source_target_pairs={{0,1},{1,2},{2,3},{3,4},{4,5},{5,6},{6,7},{7,8},{8,9},{9,10},{10,1... | collective-permute-start | bytes 208904 | tf_op jit(solution)/shard_map/ppermute | solution.py:36
  34.6 4.3 %collective-permute-start.1 = (bf16[17,4,2,256]{3,2,1,0:T(2,128)(2,1)S(1)}, bf16[17,4,2,256]{3,2,1,0:T(2,128)(2,1)S(1)}, u32[]{:S(2)}, u32[]{:S(2)}) collective-permute-start(bf16[17,4,2,256]{3,2,1,0:T(2,128)(2,1)S(1)} %get-tuple-element.62), channel_id=1, source_target_pairs={{1,0},{2,1},{3,2},{4,3},{5,4},{6,5},{7,6},{8,7},{9,8},{10,9},{11,1... | collective-permute-start | bytes 208904 | tf_op jit(solution)/shard_map/ppermute | solution.py:37
  36.4 2.5 copy-start.48
  38.9 0.6 copy-start.49
  39.8 0.7 copy-start.1
  94.3 6.4 %copy-start.2 = (bf16[3,3,3,256,256]{4,3,2,1,0:T(8,128)(2,1)S(1)}, bf16[3,3,3,256,256]{4,3,2,1,0:T(8,128)(2,1)}, u32[]{:S(2)}) copy-start(bf16[3,3,3,256,256]{4,3,2,1,0:T(8,128)(2,1)} %all-gather.2.cloned.1.call-done) | copy-start | bytes 10616836
  94.3 6.5 %copy-start.25 = (bf16[408,256]{1,0:T(8,128)(2,1)S(1)}, bf16[408,256]{1,0:T(8,128)(2,1)}, u32[]{:S(2)}) copy-start(bf16[408,256]{1,0:T(8,128)(2,1)} %reshape.233) | copy-start | bytes 626692
  94.3 6.7 %copy-start.24 = (bf16[408,256]{1,0:T(8,128)(2,1)S(1)}, bf16[408,256]{1,0:T(8,128)(2,1)}, u32[]{:S(2)}) copy-start(bf16[408,256]{1,0:T(8,128)(2,1)} %reshape.234) | copy-start | bytes 626692
  94.3 6.9 %copy-start.23 = (bf16[408,256]{1,0:T(8,128)(2,1)S(1)}, bf16[408,256]{1,0:T(8,128)(2,1)}, u32[]{:S(2)}) copy-start(bf16[408,256]{1,0:T(8,128)(2,1)} %reshape.235) | copy-start | bytes 626692
  95.7 5.8 %copy-start.22 = (bf16[408,256]{1,0:T(8,128)(2,1)S(1)}, bf16[408,256]{1,0:T(8,128)(2,1)}, u32[]{:S(2)}) copy-start(bf16[408,256]{1,0:T(8,128)(2,1)} %reshape.236) | copy-start | bytes 626692
  98.2 3.6 %copy-start.21 = (bf16[408,256]{1,0:T(8,128)(2,1)S(1)}, bf16[408,256]{1,0:T(8,128)(2,1)}, u32[]{:S(2)}) copy-start(bf16[408,256]{1,0:T(8,128)(2,1)} %reshape.237) | copy-start | bytes 626692
  99.5 2.5 copy-start.20
  100.8 1.5 copy-start.19
  101.0 1.5 copy-start.18
  101.3 1.5 copy-start.17
  101.5 1.5 copy-start.15
  101.8 1.5 copy-start.12
  102.0 1.5 copy-start.10
  102.3 1.5 copy-start.9
  102.5 1.5 copy-start.8
  102.8 1.5 copy-start.7
  103.0 1.5 copy-start.6
  103.3 1.5 copy-start.5
  103.5 1.5 copy-start.4
  103.8 1.5 copy-start.13
  104.0 1.5 copy-start.16
  104.5 1.2 copy-start.14
  104.8 1.2 copy-start.11
  114.2 56.9 %copy-start = (bf16[16,3,3,3,16,256]{5,4,3,2,1,0:T(8,128)(2,1)}, bf16[16,3,3,3,16,256]{5,4,3,2,1,0:T(8,128)(2,1)S(1)}, u32[]{:S(2)}) copy-start(bf16[16,3,3,3,16,256]{5,4,3,2,1,0:T(8,128)(2,1)S(1)} %all-to-all-done.2) | copy-start | bytes 10616836
  114.9 62.2 %all-to-all-start.1 = ((f32[16,1,64]{2,1,0:T(1,128)}), f32[16,1,64]{2,1,0:T(1,128)S(1)}, u32[]{:S(2)}, u32[]{:S(2)}) async-start(f32[16,1,64]{2,1,0:T(1,128)} %broadcast_in_dim.54), calls=%async_computation.1 | async-start | bytes 16384 | tf_op jit(solution)/shard_map/all_to_all | solution.py:13
  227.9 5.8 %copy-start.47 = (bf16[272,256]{1,0:T(8,128)(2,1)S(1)}, bf16[272,256]{1,0:T(8,128)(2,1)}, u32[]{:S(2)}) copy-start(bf16[272,256]{1,0:T(8,128)(2,1)} %reshape.266) | copy-start | bytes 417796
  227.9 6.0 %copy-start.46 = (bf16[272,256]{1,0:T(8,128)(2,1)S(1)}, bf16[272,256]{1,0:T(8,128)(2,1)}, u32[]{:S(2)}) copy-start(bf16[272,256]{1,0:T(8,128)(2,1)} %reshape.267) | copy-start | bytes 417796
  227.9 6.2 %copy-start.45 = (bf16[272,256]{1,0:T(8,128)(2,1)S(1)}, bf16[272,256]{1,0:T(8,128)(2,1)}, u32[]{:S(2)}) copy-start(bf16[272,256]{1,0:T(8,128)(2,1)} %reshape.268) | copy-start | bytes 417796
  227.9 6.4 %copy-start.44 = (bf16[272,256]{1,0:T(8,128)(2,1)S(1)}, bf16[272,256]{1,0:T(8,128)(2,1)}, u32[]{:S(2)}) copy-start(bf16[272,256]{1,0:T(8,128)(2,1)} %reshape.269) | copy-start | bytes 417796
  227.9 6.7 %copy-start.43 = (bf16[272,256]{1,0:T(8,128)(2,1)S(1)}, bf16[272,256]{1,0:T(8,128)(2,1)}, u32[]{:S(2)}) copy-start(bf16[272,256]{1,0:T(8,128)(2,1)} %reshape.270) | copy-start | bytes 417796
  229.1 5.7 %copy-start.42 = (bf16[272,256]{1,0:T(8,128)(2,1)S(1)}, bf16[272,256]{1,0:T(8,128)(2,1)}, u32[]{:S(2)}) copy-start(bf16[272,256]{1,0:T(8,128)(2,1)} %reshape.271) | copy-start | bytes 417796
  230.2 4.8 %copy-start.41 = (bf16[272,256]{1,0:T(8,128)(2,1)S(1)}, bf16[272,256]{1,0:T(8,128)(2,1)}, u32[]{:S(2)}) copy-start(bf16[272,256]{1,0:T(8,128)(2,1)} %reshape.272) | copy-start | bytes 417796
  231.4 3.8 %copy-start.40 = (bf16[272,256]{1,0:T(8,128)(2,1)S(1)}, bf16[272,256]{1,0:T(8,128)(2,1)}, u32[]{:S(2)}) copy-start(bf16[272,256]{1,0:T(8,128)(2,1)} %reshape.273) | copy-start | bytes 417796
  232.5 2.9 %copy-start.39 = (bf16[272,256]{1,0:T(8,128)(2,1)S(1)}, bf16[272,256]{1,0:T(8,128)(2,1)}, u32[]{:S(2)}) copy-start(bf16[272,256]{1,0:T(8,128)(2,1)} %reshape.274) | copy-start | bytes 417796
  233.7 2.0 copy-start.38
  233.9 2.0 copy-start.37
  234.1 2.0 copy-start.36
  234.4 2.0 copy-start.35
  234.6 2.0 copy-start.34
  234.8 2.0 copy-start.33
  235.0 2.0 copy-start.32
  235.2 2.0 copy-start.31
  235.4 2.0 copy-start.30
  235.7 2.0 copy-start.29
  235.9 1.9 copy-start.27
  236.1 1.9 copy-start.28
  236.3 1.9 copy-start.26
  236.8 3.5 %copy-start.50 = (f32[256]{0:T(256)S(1)}, f32[256]{0:T(256)}, u32[]{:S(2)}) copy-start(f32[256]{0:T(256)} %param.17) | copy-start | bytes 3076
  237.0 13.1 %copy-start.51 = (f32[4]{0:T(128)S(1)}, f32[4]{0:T(128)}, u32[]{:S(2)}) copy-start(f32[4]{0:T(128)} %get-tuple-element.67) | copy-start | bytes 52
  237.0 13.1 %copy-start.52 = (f32[4]{0:T(128)S(1)}, f32[4]{0:T(128)}, u32[]{:S(2)}) copy-start(f32[4]{0:T(128)} %get-tuple-element.68) | copy-start | bytes 52
  241.2 8.8 %collective-permute-start.2 = (bf16[4,4,4,256]{3,2,1,0:T(4,128)(2,1)S(1)}, bf16[4,4,4,256]{3,2,1,0:T(4,128)(2,1)S(1)}, u32[]{:S(2)}, u32[]{:S(2)}) collective-permute-start(bf16[4,4,4,256]{3,2,1,0:T(4,128)(2,1)S(1)} %slice.536), channel_id=1, source_target_pairs={{0,16},{16,32},{32,48},{48,64},{64,80},{80,96},{96,112},{112,128},... | collective-permute-start | bytes 98312 | tf_op jit(solution)/shard_map/ppermute | solution.py:45
Sparse Core Ops, SparseCore 0:
  9.4 81.4 all-gather.1
